TPU v7x, 256 devices: a 8x8x2 block of a 8x8x16 slice. The times are simulated.
256 devices in a mesh: parts: 2 (over z), wide: 128 (over y, x, core).
Axes of the slice: x: 8, y: 8, z: 2, core: 2. Of those that a mesh axis runs over, the one named last changes fastest.
The devices are a block of a 8x8x16 slice.
Arguments:
- a_rows: bfloat16 [327680, 2048], P(('parts', 'wide')), parts along dimension 0, may hold values from -6 to 6
- xa_panel: bfloat16 [4096, 256], P(('parts', 'wide')), parts along dimension 0, may hold values from -0.125 to 0.125
- za_panel: bfloat16 [4096, 256], P(('parts', 'wide')), parts along dimension 0, may hold values from -0.125 to 0.125
- send_order: int32 [256, 1280], P(('parts', 'wide')), parts along dimension 0, may hold values from 0 to 1279, each once within a row
- recv_order: int32 [256, 1280], P(('parts', 'wide')), parts along dimension 0, may hold values from 0 to 1279, each once within a row
- shift: float32 [128], P('parts'), parts along dimension 0, may hold values from 1 to 8
- resident: bfloat16 [327680, 1024], P(('parts', 'wide')), parts along dimension 0, may hold values from -6 to 6
Outputs:
- factored: float32 [327680, 256], P(('parts', 'wide')), parts along dimension 0
- updated: bfloat16 [327680, 1024], P(('parts', 'wide')), parts along dimension 0
- pivots: float32 [128], P('parts'), parts along dimension 0
There are 2 independent parts, one for each index of `parts`. A program takes and returns all parts, laid end to end along the dimension named above; each array names one. Nothing has to cross between parts.
Inputs may be any that keep to these rules, and one draw needn't show every extreme that they name: Each row of send_order is a permutation of the local constraint rows. Each row of recv_order is a permutation of the received slots.
All inputs are finite; a program needn't handle non-finite values.
Results may differ from a plain program's by a relative error of at most 0.0004.
Values may be sent and summed in bfloat16 or wider, within the bound.
A program may use at most 64 MiB of HBM per device.

v0:
```python
import jax
import jax.numpy as jnp
from jax import lax
from jax.sharding import PartitionSpec as P

COLS = 256
PANEL = 64
RES = 1024


def side_by_side(arrays, axis, dim, along):
    both = jnp.concatenate(arrays, axis=along)
    whole, at, done = (lax.all_gather(both, axis, axis=dim, tiled=True), 0, [])
    for a in arrays:
        done.append(lax.slice_in_dim(whole, at, at + a.shape[along], axis=along))
        at += a.shape[along]
    return tuple(done)


def factor(block, shift):
    extent = block.shape[0]
    positions = jnp.arange(extent)
    mirrored = jnp.tril(block) + jnp.tril(block, -1).T
    magnitude = jnp.sum(jnp.abs(mirrored), axis=1)
    is_diag = positions[:, None] == positions[None, :]
    work = jnp.where(is_diag, (shift + magnitude)[:, None], mirrored)

    def step(column_index, carry):
        matrix, lower, pivots = carry
        column = lax.dynamic_slice_in_dim(matrix, column_index, 1, 1)[:, 0]
        pivot = jnp.sum(jnp.where(positions == column_index, column, 0.0))
        below = jnp.where(positions > column_index, column / pivot, 0.0)
        matrix = matrix - pivot * below[:, None] * below[None, :]
        unit = jnp.where(positions == column_index, 1.0, 0.0)
        lower = lower + (below + unit)[:, None] * unit[None, :]
        pivots = pivots + unit * pivot
        return (matrix, lower, pivots)

    start = (work, jnp.zeros_like(work), jnp.zeros_like(shift))
    matrix, lower, pivots = lax.fori_loop(0, extent, step, start)
    return (lower, pivots)


def cyclic_order(gathered, group, blocks_held):
    return (
        gathered.reshape(group, blocks_held, PANEL, PANEL)
        .transpose(1, 0, 2, 3)
        .reshape(group * blocks_held * PANEL, PANEL)
    )


def on_device(a_rows, xa_panel, za_panel, send_order, recv_order, shift, resident):
    row_count = a_rows.shape[0]
    group = lax.axis_size("wide")
    my_index = lax.axis_index("wide")
    pieces = side_by_side((xa_panel, za_panel), "wide", 0, 1)
    first = jnp.dot(a_rows, pieces[0], preferred_element_type=jnp.float32)
    second = jnp.dot(a_rows, pieces[1], preferred_element_type=jnp.float32)
    schur = first * second
    outgoing = schur[send_order[0]]
    arrival = recv_order[0]
    lead = lax.all_to_all(outgoing[:, :PANEL], "wide", split_axis=0, concat_axis=0, tiled=True)[
        arrival
    ]
    rest = lax.all_to_all(outgoing[:, PANEL:], "wide", split_axis=0, concat_axis=0, tiled=True)[
        arrival
    ]
    needed = COLS + RES
    blocks_held = -(-needed // (PANEL * group))
    leading = lax.all_gather(lead[: blocks_held * PANEL], "wide", axis=0, tiled=True)
    leading = cyclic_order(leading, group, blocks_held)
    block = leading[:PANEL]
    lower, pivots = factor(block, shift)
    identity = jnp.eye(PANEL, dtype=jnp.float32)
    inverse = lax.linalg.triangular_solve(
        lower, identity, left_side=True, lower=True, unit_diagonal=True
    )
    scaled = jnp.dot(lead, inverse.T, precision=lax.Precision.HIGHEST)
    local_rows = jnp.arange(row_count)
    global_rows = (local_rows // PANEL * group + my_index) * PANEL + local_rows % PANEL
    columns_l = scaled / pivots[None, :]
    top = jnp.where(my_index == 0, lower, columns_l[:PANEL])
    panel = jnp.concatenate([top, columns_l[PANEL:]], axis=0)
    tail = jnp.dot(leading[PANEL:needed], inverse.T, precision=lax.Precision.HIGHEST)
    update = jnp.dot(panel, tail.T, precision=lax.Precision.HIGHEST)
    keep = (global_rows >= PANEL)[:, None]
    formed = rest - jnp.where(keep, update[:, : COLS - PANEL], 0.0)
    factored = jnp.concatenate([panel, formed], axis=1)
    updated = (
        resident.astype(jnp.float32) - jnp.where(keep, update[:, COLS - PANEL :], 0.0)
    ).astype(jnp.bfloat16)
    return (factored, updated, pivots)


def solution(mesh):
    placed = (
        P(("parts", "wide"), None),
        P(("parts", "wide"), None),
        P(("parts", "wide"), None),
        P(("parts", "wide"), None),
        P(("parts", "wide"), None),
        P("parts"),
        P(("parts", "wide"), None),
    )
    return jax.shard_map(
        on_device,
        mesh=mesh,
        in_specs=placed,
        out_specs=(P(("parts", "wide"), None), P(("parts", "wide"), None), P("parts")),
        check_vma=False,
    )
```

profile of v0, /device:TPU:513, one launch (start us, length us, event | category | flops | bytes accessed | tf_op | source)
XLA Modules:
  0.0 500.6 jit_solution(2949445257004039093)
XLA Ops:
  7.2 1.3 pad_maximum_fusion.2
  8.6 0.7 fusion.29
  9.4 100.5 %all-gather.3.cloned.1.call-done = bf16[2048,512]{1,0:T(8,128)(2,1)} async-done(((bf16[16,512]{1,0:T(8,128)(2,1)}), bf16[2048,512]{1,0:T(8,128)(2,1)}) %all-gather.3.cloned.1.call-update) | async-done | bytes 2097168 | tf_op jit(solution)/shard_map/all_gather | solution.py:13
  109.9 4.5 fusion.9
  114.9 1.6 fusion.7
  116.9 3.2 gather_fusion
  120.2 1.2 reshape.172
  121.3 11.7 %all-to-all-start = ((f32[128,1,640]{2,1,0:T(1,128)}), f32[128,1,640]{2,1,0:T(1,128)S(1)}, u32[]{:S(2)}, u32[]{:S(2)}) async-start(f32[128,1,640]{2,1,0:T(1,128)} %reshape.172), calls=%async_computation | async-start | bytes 655360 | tf_op jit(solution)/shard_map/all_to_all | solution.py:62
  133.4 15.3 %all-to-all-done = f32[128,1,640]{2,1,0:T(1,128)S(1)} async-done(((f32[128,1,640]{2,1,0:T(1,128)}), f32[128,1,640]{2,1,0:T(1,128)S(1)}, u32[]{:S(2)}, u32[]{:S(2)}) %all-to-all-start) | async-done | bytes 327712 | tf_op jit(solution)/shard_map/all_to_all | solution.py:62
  149.2 1.4 reduce.5
  150.9 2.4 gather_fusion.1
  154.8 2.3 reshape.170
  157.2 7.5 %all-to-all-start.1 = ((f32[128,1,1920]{2,1,0:T(1,128)}), f32[128,1,1920]{2,1,0:T(1,128)S(1)}, u32[]{:S(2)}, u32[]{:S(2)}) async-start(f32[128,1,1920]{2,1,0:T(1,128)} %reshape.170), calls=%async_computation.1 | async-start | bytes 1966080 | tf_op jit(solution)/shard_map/all_to_all | solution.py:65
  164.7 4.4 copy.34
  169.1 25.2 %all-to-all-done.1 = f32[128,1,1920]{2,1,0:T(1,128)S(1)} async-done(((f32[128,1,1920]{2,1,0:T(1,128)}), f32[128,1,1920]{2,1,0:T(1,128)S(1)}, u32[]{:S(2)}, u32[]{:S(2)}) %all-to-all-start.1) | async-done | bytes 983072 | tf_op jit(solution)/shard_map/all_to_all | solution.py:65
  194.3 3.0 reduce.4
  197.3 0.7 reshape.171
  198.2 3.2 gather_fusion.2
  201.8 40.4 %all-gather.5.cloned.1.call-done = f32[8192,64]{1,0:T(8,128)} async-done(((f32[64,64]{1,0:T(8,128)}), f32[8192,64]{1,0:T(8,128)}) %all-gather.5.cloned.1.call-update) | async-done | bytes 2097168 | tf_op jit(solution)/shard_map/all_gather | solution.py:70
  242.2 0.8 slice.58
  243.1 0.9 abs_reduce_fusion
  244.0 0.8 fusion.16
  244.8 219.3 %while.19 = (s32[]{:T(128)}, f32[64,64]{0,1:T(8,128)S(1)}, f32[64,64]{1,0:T(8,128)S(1)}, f32[64]{0:T(128)S(1)}, s32[]{:T(128)}, /*index=5*/s32[]{:T(128)}) while((s32[]{:T(128)}, f32[64,64]{0,1:T(8,128)S(1)}, f32[64,64]{1,0:T(8,128)S(1)}, f32[64]{0:T(128)S(1)}, s32[]{:T(128)}, /*index=5*/s32[]{:T(128)}) %tuple.48), condition=%wide.region_3.4_spmd.clone.clone, body=%wide.region_1.3_spmd.clone.clone.sunk | while | flops 21762 | bytes 72560 | solution.py:40
  464.3 4.9 custom-call.3
  469.4 0.8 convolution_divide_fusion
  470.6 1.9 fusion.12
  472.5 5.4 %fusion.31 = f32[1280,1216]{0,1:T(8,128)S(1)} fusion(f32[1280,64]{0,1:T(8,128)S(1)} %pad_maximum_fusion.1, f32[1216,64]{0,1:T(8,128)S(1)} %fusion.12), kind=kOutput, calls=%fused_computation.67 | convolution fusion | flops 1195376640 | bytes 6864896 | tf_op jit(solution)/shard_map/dot_general | solution.py:85
  477.9 2.6 copy-done
  480.7 1.2 pad_maximum_fusion
  481.8 2.9 copy.35
  484.7 4.6 fusion.6
  489.3 4.4 copy.36
  (496 shorter events, 221.8 us)
Async XLA Ops:
  7.2 102.7 %all-gather.3.cloned.1.call-start = ((), (), s32[]{:S(2)}) async-start(), calls=%async_computation.2 | async-start | bytes 2113536 | tf_op jit(solution)/shard_map/all_gather | solution.py:13
  109.9 4.5 copy-start.6
  109.9 5.0 copy-start.7
  120.1 13.3 %copy-start.5 = (s32[1,1280]{1,0:T(1,128)S(1)}, s32[1,1280]{1,0:T(1,128)}, u32[]{:S(2)}) copy-start(s32[1,1280]{1,0:T(1,128)} %param.13) | copy-start | bytes 15364
  121.3 27.4 %all-to-all-start = ((f32[128,1,640]{2,1,0:T(1,128)}), f32[128,1,640]{2,1,0:T(1,128)S(1)}, u32[]{:S(2)}, u32[]{:S(2)}) async-start(f32[128,1,640]{2,1,0:T(1,128)} %reshape.172), calls=%async_computation | async-start | bytes 655360 | tf_op jit(solution)/shard_map/all_to_all | solution.py:62
  133.1 109.2 %all-gather.5.cloned.1.call-start = ((), (), s32[]{:S(2)}) async-start(), calls=%async_computation.3 | async-start | bytes 4227072 | tf_op jit(solution)/shard_map/all_gather | solution.py:70
  153.3 0.9 copy-start.2
  157.2 37.1 %all-to-all-start.1 = ((f32[128,1,1920]{2,1,0:T(1,128)}), f32[128,1,1920]{2,1,0:T(1,128)S(1)}, u32[]{:S(2)}, u32[]{:S(2)}) async-start(f32[128,1,1920]{2,1,0:T(1,128)} %reshape.170), calls=%async_computation.1 | async-start | bytes 1966080 | tf_op jit(solution)/shard_map/all_to_all | solution.py:65
  201.4 42.5 %copy-start.8 = (f32[64]{0:T(128)S(1)}, f32[64]{0:T(128)}, u32[]{:S(2)}) copy-start(f32[64]{0:T(128)} %param.14) | copy-start | bytes 772
  201.4 268.0 %copy-start.3 = (f32[1280,64]{1,0:T(8,128)S(1)}, f32[1280,64]{1,0:T(8,128)}, u32[]{:S(2)}) copy-start(f32[1280,64]{1,0:T(8,128)} %copy-done.2) | copy-start | bytes 983044
  464.1 13.8 %copy-start.4 = (f32[64]{0:T(128)}, f32[64]{0:T(128)S(1)}, u32[]{:S(2)}) copy-start(f32[64]{0:T(128)S(1)} %get-tuple-element.142) | copy-start | bytes 772
  477.9 2.6 copy-start
  480.7 4.0 copy-start.1
Sparse Core Ops, SparseCore 0:
  11.2 98.6 all-gather.2
  154.3 87.8 all-gather.4
where the time goes:
time: 504 us; the launch traced here: 501 us
  other arithmetic  236 us (47%)
  waiting for transfers between devices  182 us (36%)
  local copies, waits for them, and re-layouts  32 us (6%)
  starting transfers between devices  19.5 us (4%)
  matrix products  14.5 us (3%)
  between operations  14.4 us (3%)
    all_gather x1, waiting for transfers between devices, side_by_side(): whole, at, done = (lax.all_gather(both, axis, axis=dim, tiled=True), 0, [])  101 us
    add x64, other arithmetic, step(): pivots = pivots + unit * pivot  42.5 us
    mul x64, other arithmetic, step(): lower = lower + (below + unit)[:, None] * unit[None, :]  42.1 us
    select_n x64, other arithmetic, step(): below = jnp.where(positions > column_index, column / pivot, 0.0)  41.9 us
    mul x64, other arithmetic, step(): matrix = matrix - pivot * below[:, None] * below[None, :]  41.6 us
    all_gather x1, waiting for transfers between devices, on_device(): lax.all_gather(lead[:blocks_held * PANEL], 'wide', axis=0, tiled=True)  40.4 us
    reduce_sum x64, other arithmetic, step(): pivot = jnp.sum(jnp.where(positions == column_index, column, 0.0))  38.8 us
    all_to_all x1, waiting for transfers between devices, on_device(): lax.all_to_all(outgoing[:, PANEL:], 'wide', split_axis=0, concat_axis=0,...  25.2 us
  transfers between devices with their start and end apart: 4, of which 4 were waited for; matrix products, arithmetic and copies ran while one was open for 3% of the time, Pallas kernels for 0%

commit v1 on v0

v1 whole, which is shorter than its diff:
```python
import functools
import math

import jax
import jax.numpy as jnp
from jax import lax
from jax.experimental import pallas as pl
from jax.experimental.pallas import tpu as pltpu
from jax.sharding import PartitionSpec as P

PANEL = 64
LANES = 128
Q_MAX = 32767.0
F32 = jnp.float32
BF16 = jnp.bfloat16


def lane_iota(shape):
    return lax.broadcasted_iota(jnp.int32, shape, len(shape) - 1)


def exchange_kernel(
    n, n_lead,
    a_hbm, xa_hbm, za_hbm, send_ref, slot_a_ref, slot_b_ref,
    stored_a, stored_b, leading,
    a_vmem, gathered, sa, sr, sb, lead_out, rest_f, rest_out,
    lead_in, rest_in, rest_g, both_a, first_rows, leading_src,
    a_sem, own_sem, ag_send, ag_recv1, ag_recv2, ag_recv3,
    lead_send, lead_recv, rest_send, rest_recv,
    tree_send1, tree_send2, tree_send3, tree_recv1, tree_recv2, tree_recv3,
):
    side = math.isqrt(n // 2)
    rows = a_vmem.shape[0]
    per = rows // n
    pair = per // 2
    me = lax.axis_index("wide")
    core = lax.rem(me, 2)
    chip = lax.div(me, 2)
    x = lax.rem(chip, side)
    y = lax.div(chip, side)
    u = x + core * (y - x)
    v = y + core * (x - y)
    sibling = chip * 2 + 1 - core

    def chip_of(uu, vv):
        return vv * (side - (side - 1) * core) + uu * (1 + (side - 1) * core)

    def wrap(value):
        return lax.rem(value + 2 * side, side)

    def remote(src, dst, send, recv, target):
        pltpu.make_async_remote_copy(
            src_ref=src, dst_ref=dst, send_sem=send, recv_sem=recv,
            device_id={"wide": target}, device_id_type=pl.DeviceIdType.MESH,
        ).start()

    def await_bytes(ref, sem):
        pltpu.make_async_copy(ref, ref, sem).wait()

    a_copy = pltpu.make_async_copy(a_hbm, a_vmem, a_sem)
    a_copy.start()
    own_x = pltpu.make_async_copy(xa_hbm, gathered.at[chip, core, 0], own_sem.at[0])
    own_z = pltpu.make_async_copy(za_hbm, gathered.at[chip, core, 1], own_sem.at[1])
    own_x.start()
    own_z.start()

    barrier = pltpu.get_barrier_semaphore()
    partners = [chip_of(wrap(u + i), v) * 2 + core for i in range(1, side)]
    partners += [chip_of(u, wrap(v + d)) * 2 + core for d in (1, -1)]
    partners += [sibling]
    for partner in partners:
        pl.semaphore_signal(
            barrier, inc=1, device_id={"wide": partner}, device_id_type=pl.DeviceIdType.MESH
        )
    rest_f[:, 3 * pair :, :] = jnp.zeros((n, 16 - 3 * pair, LANES), F32)
    own_x.wait()
    own_z.wait()
    pl.semaphore_wait(barrier, len(partners))

    def send_block(block_chip, target, send, recv):
        block = gathered.at[block_chip, core]
        remote(block, block, send, recv, target)

    half = side // 2
    for i in sorted(range(1, side), key=lambda i: -min(i, side - i)):
        send_block(chip, chip_of(wrap(u + i), v) * 2 + core, ag_send.at[0], ag_recv1)
    await_bytes(gathered.at[0 : side - 1, 0], ag_recv1)
    for step in range(1, half + 2):
        for part in range(2):
            for way, direction in enumerate((1, -1)):
                last_ok = part == way
                if step == half + 1 and not last_ok:
                    continue
                if step > 1:
                    await_bytes(gathered.at[0:half, 0], ag_recv2.at[way, step - 2, part])
                row = wrap(v - direction * (step - 1))
                blocks = [chip_of(part * half + k, row) for k in range(half)]
                if step < half or (step == half and last_ok):
                    target = chip_of(u, wrap(v + direction)) * 2 + core
                    for block in blocks:
                        send_block(block, target, ag_send.at[1], ag_recv2.at[way, step - 1, part])
                if step > 1 or way == 0:
                    for block in blocks:
                        send_block(block, sibling, ag_send.at[2], ag_recv3)
    await_bytes(gathered.at[:, 0], ag_recv3)
    a_copy.wait()

    tile = rows // 4
    depth = a_vmem.shape[1]

    def product(t, _):
        at = pl.ds(pl.multiple_of(t * tile, tile), tile)
        lhs = a_vmem[at, :]
        cols = gathered.shape[-1]
        one = jnp.dot(lhs, gathered[:, :, 0].reshape(depth, cols), preferred_element_type=F32)
        two = jnp.dot(lhs, gathered[:, :, 1].reshape(depth, cols), preferred_element_type=F32)
        schur = one * two
        sa[at, :] = schur[:, :LANES]
        sr[at, :] = pltpu.roll(schur[:, :LANES], PANEL, 1)
        sb[at, :] = schur[:, LANES:]
        return 0

    lax.fori_loop(0, 4, product, 0)

    low = lane_iota((1, LANES)) < PANEL

    def pack_lead(e, _):
        for k in range(pair):
            one = send_ref[0, e * per + k]
            two = send_ref[0, e * per + pair + k]
            lead_out[e, pl.ds(k, 1), :] = jnp.where(
                low, sa[pl.ds(one, 1), :], sr[pl.ds(two, 1), :]
            )
        return 0

    lax.fori_loop(0, n, pack_lead, 0)

    def send_to(e, source, target_ref, send, recv):
        @pl.when(e != me)
        def _():
            remote(source.at[e], target_ref.at[me], send, recv, e)

    def lead_first(i, _):
        send_to(lax.rem(me + i, n_lead), lead_out, lead_in, lead_send, lead_recv)
        return 0

    def lead_other(i, _):
        e = n_lead + lax.rem(me + i, n - n_lead)
        send_to(e, lead_out, lead_in, lead_send, lead_recv)
        return 0

    lax.fori_loop(0, n_lead, lead_first, 0)
    lax.fori_loop(0, n - n_lead, lead_other, 0)
    lead_in[me] = lead_out[me]

    def pack_rest(e, _):
        for k in range(pair):
            one = send_ref[0, e * per + k]
            two = send_ref[0, e * per + pair + k]
            rest_f[e, pl.ds(k, 1), :] = sb[pl.ds(one, 1), :]
            rest_f[e, pl.ds(pair + k, 1), :] = sb[pl.ds(two, 1), :]
            rest_f[e, pl.ds(2 * pair + k, 1), :] = jnp.where(
                low, sr[pl.ds(one, 1), :], sa[pl.ds(two, 1), :]
            )
        return 0

    lax.fori_loop(0, n, pack_rest, 0)

    def quantize(i, _):
        at = pl.ds(i * 8, 8)
        values = rest_f[at]
        largest = jnp.max(jnp.abs(values), axis=1, keepdims=True)
        power = jnp.floor(jnp.log2(jnp.maximum(largest, 1e-30))) + 1.0
        scale = Q_MAX / jnp.exp2(power)
        coded = jnp.clip(jnp.round(values * scale), -Q_MAX, Q_MAX)
        spot = lax.broadcasted_iota(jnp.int32, values.shape, 1)
        coded = jnp.where(spot == 3 * pair, power, coded)
        rest_out[at] = coded.astype(jnp.int32).astype(jnp.int16)
        return 0

    lax.fori_loop(0, n // 8, quantize, 0)

    await_bytes(lead_in.at[0 : n - 1], lead_recv)

    def spread_lead(i, _):
        at = pl.ds(i * 8, 8)
        values = lead_in[at]
        both_a[0, at, 0:pair] = values
        both_a[1, at, 0:pair] = pltpu.roll(values, PANEL, 2)
        return 0

    lax.fori_loop(0, n // 8, spread_lead, 0)
    flat_a = both_a.reshape(2 * n * 8, LANES)

    def first(q, _):
        first_rows[pl.ds(q, 1), :] = flat_a[pl.ds(slot_a_ref[0, q], 1), :]
        return 0

    lax.fori_loop(0, PANEL, first, 0)
    hp = PANEL // 2
    leading_src[...] = jnp.where(
        low, first_rows[0:hp, :], pltpu.roll(first_rows[hp:PANEL, :], PANEL, 1)
    )

    group = 2 * side
    levels = -(-n_lead // group)

    @pl.when(me < n_lead)
    def _():
        leading[me] = leading_src[...]
        for i in range(1, side):
            target = (wrap(y + i) * side + x) * 2 + core
            remote(leading_src, leading.at[me], tree_send1, tree_recv1.at[y], target)

    for m in range(levels):
        e = m * group + 2 * x + core

        @pl.when(e < n_lead)
        def _(m=m, e=e):
            @pl.when(y != m)
            def _():
                await_bytes(leading.at[0], tree_recv1.at[m])

            for i in range(1, side):
                target = (y * side + wrap(x + i)) * 2 + core
                remote(leading.at[e], leading.at[e], tree_send2.at[m], tree_recv2.at[e], target)
            remote(leading.at[e], leading.at[e], tree_send3.at[e], tree_recv3.at[e], sibling)

    def rest_all(i, _):
        send_to(lax.rem(me + i, n), rest_out, rest_in, rest_send, rest_recv)
        return 0

    lax.fori_loop(1, n, rest_all, 0)
    rest_in[me] = rest_out[me]

    for m in range(levels):
        for i in range(1, side):
            e = m * group + 2 * wrap(x + i) + core

            @pl.when(e < n_lead)
            def _(e=e):
                await_bytes(leading.at[0], tree_recv2.at[e])
                remote(leading.at[e], leading.at[e], tree_send3.at[e], tree_recv3.at[e], sibling)

    def from_sibling(e, _):
        @pl.when(lax.rem(e, 2) != core)
        def _():
            await_bytes(leading.at[0], tree_recv3.at[e])

        return 0

    lax.fori_loop(0, n_lead, from_sibling, 0)

    await_bytes(rest_in.at[0 : n - 1], rest_recv)

    def spread_rest(i, _):
        at = pl.ds(i * 8, 8)
        coded = rest_in[at].astype(jnp.int32).astype(F32)
        power = coded[:, 3 * pair : 3 * pair + 1]
        values = coded * (jnp.exp2(power) / Q_MAX)
        rest_g[at] = values
        mid = values[:, 2 * pair : 3 * pair]
        kept = lane_iota(mid.shape) < PANEL
        both_a[0, at, 0:pair] = jnp.where(kept, both_a[0, at, 0:pair], pltpu.roll(mid, PANEL, 2))
        both_a[1, at, 0:pair] = jnp.where(kept, both_a[1, at, 0:pair], mid)
        return 0

    lax.fori_loop(0, n // 8, spread_rest, 0)
    flat_b = rest_g.reshape(n * 16, LANES)

    def place(i, _):
        for k in range(8):
            q = i * 8 + k
            stored_a[pl.ds(q, 1), :] = flat_a[pl.ds(slot_a_ref[0, q], 1), :]
            stored_b[pl.ds(q, 1), :] = flat_b[pl.ds(slot_b_ref[0, q], 1), :]
        return 0

    lax.fori_loop(0, rows // 8, place, 0)

    await_bytes(gathered.at[0 : side - 1, 0], ag_send.at[0])
    await_bytes(gathered.at[0 : side * (side - 1), 0], ag_send.at[1])
    await_bytes(gathered.at[:, 0], ag_send.at[2])
    await_bytes(lead_out.at[0 : n - 1], lead_send)
    await_bytes(rest_out.at[0 : n - 1], rest_send)

    @pl.when(me < n_lead)
    def _():
        await_bytes(leading.at[0 : side - 1], tree_send1)

    for m in range(levels):
        e = m * group + 2 * x + core

        @pl.when(e < n_lead)
        def _(m=m):
            await_bytes(leading.at[0 : side - 1], tree_send2.at[m])

    def to_sibling(e, _):
        @pl.when(lax.rem(e, 2) == core)
        def _():
            await_bytes(leading.at[0], tree_send3.at[e])

        return 0

    lax.fori_loop(0, n_lead, to_sibling, 0)


def exchange(n, n_lead, a_rows, xa, za, send_order, slot_a, slot_b):
    rows, depth = a_rows.shape
    cols = xa.shape[1]
    share = xa.shape[0]
    per = rows // n
    pair = per // 2
    side = math.isqrt(n // 2)
    hp = PANEL // 2
    dma = pltpu.SemaphoreType.DMA
    any_spec = pl.BlockSpec(memory_space=pl.ANY)
    smem = pl.BlockSpec(memory_space=pltpu.SMEM)
    vmem = pl.BlockSpec(memory_space=pltpu.VMEM)
    levels = -(-n_lead // (2 * side))
    return pl.pallas_call(
        functools.partial(exchange_kernel, n, n_lead),
        out_shape=(
            jax.ShapeDtypeStruct((rows, LANES), F32),
            jax.ShapeDtypeStruct((rows, LANES), F32),
            jax.ShapeDtypeStruct((n_lead, hp, LANES), F32),
        ),
        in_specs=[any_spec, any_spec, any_spec, smem, smem, smem],
        out_specs=(vmem, vmem, vmem),
        scratch_shapes=[
            pltpu.VMEM((rows, depth), BF16),
            pltpu.VMEM((n // 2, 2, 2, share, cols), BF16),
            pltpu.VMEM((rows, LANES), F32),
            pltpu.VMEM((rows, LANES), F32),
            pltpu.VMEM((rows, LANES), F32),
            pltpu.VMEM((n, pair, LANES), F32),
            pltpu.VMEM((n, 16, LANES), F32),
            pltpu.VMEM((n, 16, LANES), jnp.int16),
            pltpu.VMEM((n, pair, LANES), F32),
            pltpu.VMEM((n, 16, LANES), jnp.int16),
            pltpu.VMEM((n, 16, LANES), F32),
            pltpu.VMEM((2, n, 8, LANES), F32),
            pltpu.VMEM((PANEL, LANES), F32),
            pltpu.VMEM((hp, LANES), F32),
            dma, dma((2,)), dma((3,)), dma, dma((2, side // 2, 2)), dma,
            dma, dma, dma, dma,
            dma, dma((levels,)), dma((n_lead,)), dma((side,)), dma((n_lead,)), dma((n_lead,)),
        ],
        compiler_params=pltpu.CompilerParams(
            collective_id=0, has_side_effects=True, vmem_limit_bytes=48 * 1024 * 1024
        ),
    )(a_rows, xa, za, send_order, slot_a, slot_b)


def two_parts(values):
    high = values.astype(BF16)
    return high, (values - high.astype(F32)).astype(BF16)


def left_stack(twice):
    high, mid = two_parts(twice)
    return jnp.concatenate([high, mid], axis=1)


def right_stack(twice):
    high, mid = two_parts(twice)
    once = jnp.where(lane_iota(twice.shape) < PANEL, high.astype(F32), mid.astype(F32))
    once = once.astype(BF16)
    return jnp.concatenate([once, once], axis=1)


def dot_nt(a, b):
    return lax.dot_general(a, b, (((1,), (1,)), ((), ())), preferred_element_type=F32)


def finish_kernel(
    a_ref, b_ref, leading, shift_ref, resident_ref,
    factored_ref, updated_ref, pivots_ref,
    work, lower_ref, inverse_ref, tail_ref,
):
    step = pl.program_id(0)
    me = lax.axis_index("wide")
    tile = a_ref.shape[0]

    @pl.when(step == 0)
    def _():
        head = leading[0]
        lanes = lane_iota(head.shape)
        turned = pltpu.roll(head, PANEL, 1)
        block = jnp.concatenate([head, turned], axis=0)
        r = lax.broadcasted_iota(jnp.int32, block.shape, 0)
        c = lane_iota(block.shape)
        inside = c < PANEL
        strict = jnp.where((r > c) & inside, block, 0.0)
        pad = jnp.concatenate([strict, jnp.zeros_like(strict)], axis=0)
        mirrored = jnp.where((r >= c) & inside, block, 0.0) + pad.T[:PANEL, :]
        magnitude = jnp.sum(jnp.abs(mirrored), axis=0, keepdims=True)
        diagonal = magnitude + shift_ref[...]
        start = jnp.where(r == c, diagonal, mirrored)
        work[...] = jnp.where(inside, start, jnp.where(r == c - PANEL, 1.0, 0.0))
        lower_ref[...] = jnp.zeros_like(block)

        def eliminate(j, pivots):
            matrix = work[...]
            row = work[pl.ds(j, 1), :]
            column = jnp.sum(jnp.where(c == j, matrix, 0.0), axis=1, keepdims=True)
            first = lane_iota(row.shape) == j
            pivot = jnp.sum(jnp.where(first, row, 0.0), axis=1, keepdims=True)
            below = jnp.where(r > j, column / pivot, 0.0)
            work[...] = matrix - below * row
            lower_ref[...] += jnp.where(c == j, below + jnp.where(r == j, 1.0, 0.0), 0.0)
            return jnp.where(first, pivot, pivots)

        pivots = lax.fori_loop(0, PANEL, eliminate, jnp.ones((1, LANES), F32))
        pivots_ref[...] = pivots
        final = work[...]
        inverse = jnp.where(inside, pltpu.roll(final, PANEL, 1), final)
        inverse_ref[0:PANEL, :] = right_stack(inverse)
        inverse_ref[PANEL:, :] = jnp.zeros_like(inverse_ref[PANEL:, :])
        blocks = leading[...]
        keep = lane_iota(blocks.shape) < PANEL
        other = pltpu.roll(blocks, PANEL, 2)
        top = jnp.where(keep, blocks, other)
        bottom = jnp.where(keep, other, blocks)
        full = jnp.concatenate([top, bottom], axis=1)
        full = full.reshape(full.shape[0] * PANEL, LANES)
        tail = dot_nt(left_stack(full), inverse_ref[...])
        tail = tail + pltpu.roll(tail, PANEL, 1)
        place = lax.broadcasted_iota(jnp.int32, tail.shape, 0)
        tail_ref[...] = right_stack(jnp.where(place < PANEL, 0.0, tail))

    a = a_ref[...]
    lanes = lane_iota(a.shape)
    local = lax.broadcasted_iota(jnp.int32, a.shape, 0) + step * tile
    low = lanes < PANEL
    lead = jnp.where(low, a, pltpu.roll(a, PANEL, 1))
    scaled = dot_nt(left_stack(lead), inverse_ref[...])
    panel = scaled / pivots_ref[...]
    is_top = (local < PANEL) & (me == 0)
    fill = tile // PANEL
    lower = jnp.concatenate([lower_ref[...]] * fill, axis=0)
    panel = jnp.where(is_top, lower, panel)
    update = dot_nt(left_stack(panel + pltpu.roll(panel, PANEL, 1)), tail_ref[...])
    cols = b_ref.shape[1] + a.shape[1]

    def kept(values):
        rows_at = lax.broadcasted_iota(jnp.int32, values.shape, 0) + step * tile
        return jnp.where((rows_at < PANEL) & (me == 0), 0.0, values)

    factored_ref[:, :LANES] = jnp.where(low, panel, a - kept(update[:, :LANES]))
    factored_ref[:, LANES:] = b_ref[...] - kept(update[:, LANES:cols])
    updated_ref[...] = (resident_ref[...].astype(F32) - kept(update[:, cols:])).astype(BF16)


def finish(stored_a, stored_b, leading, shift, resident):
    rows = stored_a.shape[0]
    tile = 256
    width = resident.shape[1]
    cols = stored_a.shape[1] + stored_b.shape[1]
    n_lead = leading.shape[0]
    row_spec = lambda w: pl.BlockSpec((tile, w), lambda i: (i, 0))
    whole = lambda shape: pl.BlockSpec(shape, lambda i: (0,) * len(shape))
    return pl.pallas_call(
        finish_kernel,
        grid=(rows // tile,),
        out_shape=(
            jax.ShapeDtypeStruct((rows, cols), F32),
            jax.ShapeDtypeStruct((rows, width), BF16),
            jax.ShapeDtypeStruct((1, LANES), F32),
        ),
        in_specs=[
            row_spec(LANES), row_spec(LANES), whole(leading.shape), whole((1, LANES)),
            row_spec(width),
        ],
        out_specs=(row_spec(cols), row_spec(width), whole((1, LANES))),
        scratch_shapes=[
            pltpu.VMEM((PANEL, LANES), F32),
            pltpu.VMEM((PANEL, LANES), F32),
            pltpu.VMEM((LANES, 2 * LANES), BF16),
            pltpu.VMEM((n_lead * PANEL, 2 * LANES), BF16),
        ],
        compiler_params=pltpu.CompilerParams(vmem_limit_bytes=32 * 1024 * 1024),
    )(stored_a, stored_b, leading, shift, resident)


def on_device(n, a_rows, xa_panel, za_panel, send_order, recv_order, shift, resident):
    rows = a_rows.shape[0]
    per = rows // n
    pair = per // 2
    needed = xa_panel.shape[1] + resident.shape[1]
    n_lead = -(-needed // PANEL)
    source = recv_order // per
    slot = recv_order % per
    slot_a = (slot // pair) * (n * 8) + source * 8 + slot % pair
    slot_b = source * 16 + slot
    stored_a, stored_b, leading = exchange(
        n, n_lead, a_rows, xa_panel, za_panel, send_order, slot_a, slot_b
    )
    padded = jnp.concatenate([shift, jnp.ones_like(shift)])[None, :]
    factored, updated, pivots = finish(stored_a, stored_b, leading, padded, resident)
    return factored, updated, pivots[0, :PANEL]


def solution(mesh):
    spread = P(("parts", "wide"), None)
    return jax.shard_map(
        functools.partial(on_device, mesh.shape["wide"]),
        mesh=mesh,
        in_specs=(spread, spread, spread, spread, spread, P("parts"), spread),
        out_specs=(spread, spread, P("parts")),
        check_vma=False,
    )
```

time: 504 us -> 103 us (0.20)
  other arithmetic: 236 us -> 1.5 us
  waiting for transfers between devices: 182 us -> 0 us
  Pallas kernels: 0 us -> 97.2 us
  local copies, waits for them, and re-layouts: 32 us -> 3.25 us
  starting transfers between devices: 19.5 us -> 0 us
  matrix products: 14.5 us -> 0 us
  between operations: 14.4 us -> 0.66 us
    all_gather x2 -> x0, waiting for transfers between devices: 141 us -> none  [the longest x1 101 us: side_by_side(): whole, at, done = (lax.all_gather(both, axis, axis=dim, tiled=True), 0, [])]
    pallas_call x0 -> x2, Pallas kernels: none -> 97.2 us  [the longest x1 86.1 us: exchange(): pl.pallas_call(functools.partial(exchange_kernel, n, n_lead), out_shape=(...]
    mul x128 -> x0, other arithmetic: 83.7 us -> none  [the longest x64 42.1 us: step(): lower = lower + (below + unit)[:, None] * unit[None, :]]
    add x130 -> x2, other arithmetic: 47.3 us -> 1.5 us  [the longest x1 0.76 us: on_device(): slot_a = slot // pair * (n * 8) + source * 8 + slot % pair]
    select_n x68 -> x0, other arithmetic: 43.5 us -> none  [the longest x64 41.9 us: step(): below = jnp.where(positions > column_index, column / pivot, 0.0)]
    all_to_all x2 -> x0, waiting for transfers between devices: 40.5 us -> none  [the longest x1 25.2 us: on_device(): lax.all_to_all(outgoing[:, PANEL:], 'wide', split_axis=0, concat_axis=0,...]
    reduce_sum x65 -> x0, other arithmetic: 39.7 us -> none  [the longest x64 38.8 us: step(): pivot = jnp.sum(jnp.where(positions == column_index, column, 0.0))]
    all_to_all x2 -> x0, starting transfers between devices: 19.2 us -> none  [the longest x1 11.7 us: on_device(): lax.all_to_all(outgoing[:, :PANEL], 'wide', split_axis=0, concat_axis=0,...]
  transfers between devices with their start and end apart: 4 -> 0, of which waited for: 4 -> 0; matrix products, arithmetic and copies ran while one was open for 3% -> 0% of each run, Pallas kernels for 0% -> 0%
where the time goes in v1:
time: 103 us
  Pallas kernels  97.2 us (94%)
  local copies, waits for them, and re-layouts  3.25 us (3%)
  other arithmetic  1.5 us (1%)
    pallas_call x1, Pallas kernels, exchange(): pl.pallas_call(functools.partial(exchange_kernel, n, n_lead), out_shape=(...  86.1 us
    pallas_call x1, Pallas kernels, finish(): pl.pallas_call(finish_kernel, grid=(rows // tile,), out_shape=(jax.ShapeD...  11.1 us
    unnamed x8, local copies, waits for them, and re-layouts  2.08 us

profile of v1, /device:TPU:513, one launch (start us, length us, event | category | flops | bytes accessed | tf_op | source)
XLA Modules:
  0.0 102.6 jit_solution(15967121877994132257)
XLA Ops:
  0.6 0.7 pad_bitcast_fusion.shift_ref
  1.3 0.7 multiply_add_fusion
  2.0 0.8 fusion.slot_a_ref
  2.8 0.0 copy-start.1
  2.8 0.7 copy-done.1
  3.5 0.0 copy-start.2
  3.5 0.7 copy-done.2
  4.2 0.0 copy-start.3
  4.2 0.7 copy-done.3
  4.9 0.0 copy-start
  4.9 86.1 %shard_map.94 = (f32[1280,128]{1,0:T(8,128)S(1)}, f32[1280,128]{1,0:T(8,128)S(1)}, f32[20,32,128]{2,1,0:T(8,128)S(1)}) custom-call(bf16[1280,2048]{1,0:T(8,128)(2,1)} %a_hbm.1, bf16[16,256]{1,0:T(8,128)(2,1)S(1)} %copy-done.1, bf16[16,256]{1,0:T(8,128)(2,1)S(1)} %copy-done.2, s32[1,1280]{1,0:T(1,128)S(1)} %copy-done.3, s32[1,1280]{1,0:T(1,128)S(1)} %fusion.slot_a_ref, ...), custom_call_target="tpu_custom_call" | custom-call | tf_op jit(solution)/shard_map/pallas_call | solution.py:320
  91.0 0.0 copy-done
  91.0 11.1 %shard_map.95 = (f32[1280,256]{1,0:T(8,128)}, bf16[1280,1024]{1,0:T(8,128)(2,1)}, f32[1,128]{1,0:T(1,128)S(1)}) custom-call(f32[1280,128]{1,0:T(8,128)S(1)} %get-tuple-element.9.a_ref, f32[1280,128]{1,0:T(8,128)S(1)} %get-tuple-element.10.b_ref, f32[20,32,128]{2,1,0:T(8,128)S(1)} %get-tuple-element.11.leading, f32[1,128]{1,0:T(1,128)S(1)} %pad_bitcast_fusion.shift_ref, ...), custom_call_target="tpu_custom_call" | custom-call | tf_op jit(solution)/shard_map/pallas_call | solution.py:462
  102.1 0.5 slice_bitcast_fusion
Async XLA Ops:
  2.8 0.7 copy-start.1
  3.5 0.7 copy-start.2
  4.2 0.7 copy-start.3
  4.9 86.1 %copy-start = (bf16[1280,1024]{1,0:T(8,128)(2,1)S(1)}, bf16[1280,1024]{1,0:T(8,128)(2,1)}, u32[]{:S(2)}) copy-start(bf16[1280,1024]{1,0:T(8,128)(2,1)} %resident_ref.1) | copy-start | bytes 7864324

commit v2 on v1

v2 whole, which is shorter than its diff:
```python
import functools
import math

import jax
import jax.numpy as jnp
from jax import lax
from jax.experimental import pallas as pl
from jax.experimental.pallas import tpu as pltpu
from jax.sharding import PartitionSpec as P

PANEL = 64
LANES = 128
Q_MAX = 32767.0
F32 = jnp.float32
BF16 = jnp.bfloat16


def lane_iota(shape):
    return lax.broadcasted_iota(jnp.int32, shape, len(shape) - 1)


def u_groups(side):
    half = side // 2
    groups = [(0,)] + [(o, -o) for o in range(1, half - 1)]
    return groups + [(half - 1, 1 - half, half)]


def exchange_kernel(
    n, n_lead,
    a_hbm, xa_hbm, za_hbm, send_hbm, recv_hbm, shift_hbm,
    stored_a, stored_b, leading, work, lower_ref, pivots_ref,
    a_vmem, gathered, sa, sr, sb, lead_out, rest_f, rest_out,
    lead_in, rest_in, rest_g, both_a, first_rows, leading_src,
    shift_ref, send_ref, recv_ref, slots,
    a_sem, own_sem, order_sem, ag_send, ag_recv_u, ag_recv_v, ag_recv_s,
    lead_send, lead_recv, rest_send, rest_recv,
    tree_send1, tree_send2, tree_send3, tree_recv1, tree_recv2, tree_recv3,
):
    side = math.isqrt(n // 2)
    rows = a_vmem.shape[0]
    per = rows // n
    pair = per // 2
    me = lax.axis_index("wide")
    core = lax.rem(me, 2)
    chip = lax.div(me, 2)
    x = lax.rem(chip, side)
    y = lax.div(chip, side)
    u = x + core * (y - x)
    v = y + core * (x - y)
    sibling = chip * 2 + 1 - core
    step_u = 1 + (side - 1) * core
    step_v = side - (side - 1) * core

    def chip_of(uu, vv):
        return vv * step_v + uu * step_u

    def wrap(value):
        return lax.rem(value + 2 * side, side)

    def remote(src, dst, send, recv, target):
        pltpu.make_async_remote_copy(
            src_ref=src, dst_ref=dst, send_sem=send, recv_sem=recv,
            device_id={"wide": target}, device_id_type=pl.DeviceIdType.MESH,
        ).start()

    def await_bytes(ref, sem):
        pltpu.make_async_copy(ref, ref, sem).wait()

    own_x = pltpu.make_async_copy(xa_hbm, gathered.at[chip, core, 0], own_sem.at[0])
    own_z = pltpu.make_async_copy(za_hbm, gathered.at[chip, core, 1], own_sem.at[1])
    own_x.start()
    own_z.start()

    at_u = {o: wrap(u + o) for o in range(-(side // 2) + 1, side // 2 + 1)}
    at_v = {o: wrap(v + o) for o in range(-2, 3)}
    to_u = {o: chip_of(at_u[o], v) * 2 + core for o in at_u if o}
    to_v = {o: chip_of(u, at_v[o]) * 2 + core for o in at_v if o}
    barrier = pltpu.get_barrier_semaphore()
    partners = list(to_u.values()) + list(to_v.values()) + [sibling]
    for partner in partners:
        pl.semaphore_signal(
            barrier, inc=1, device_id={"wide": partner}, device_id_type=pl.DeviceIdType.MESH
        )
    a_copy = pltpu.make_async_copy(a_hbm, a_vmem, a_sem)
    send_copy = pltpu.make_async_copy(send_hbm, send_ref, order_sem.at[0])
    recv_copy = pltpu.make_async_copy(recv_hbm, recv_ref, order_sem.at[1])
    a_copy.start()
    send_copy.start()
    shift_copy = pltpu.make_async_copy(shift_hbm, shift_ref, order_sem.at[2])
    recv_copy.start()
    shift_copy.start()
    own_x.wait()
    own_z.wait()
    pl.semaphore_wait(barrier, len(partners))

    def send_block(block_chip, target, send, recv):
        block = gathered.at[block_chip, core]
        remote(block, block, send, recv, target)

    half = side // 2
    groups = u_groups(side)
    group_of = {o: g for g, members in enumerate(groups) for o in members}
    across = ((0, len(groups) - 1), tuple(range(1, len(groups) - 1)))
    signs = (1, -1)
    for o in sorted(to_u, key=lambda o: -abs(o)):
        send_block(chip, to_u[o], ag_send.at[0], ag_recv_u.at[group_of[o]])

    def blocks_of(g, row):
        return [chip_of(at_u[o], row) for o in groups[g]]

    def send_v(g, row, hop, way, jump):
        for block in blocks_of(g, row):
            send_block(
                block, to_v[signs[way] * jump], ag_send.at[1], ag_recv_v.at[way, hop - 1, g]
            )

    def share(g, row):
        for block in blocks_of(g, row):
            send_block(block, sibling, ag_send.at[2], ag_recv_s)

    def arrived(g, hop, way):
        await_bytes(gathered.at[0 : len(groups[g]), 0], ag_recv_v.at[way, hop - 1, g])

    for g in range(len(groups)):
        if g > 0:
            await_bytes(gathered.at[0 : len(groups[g]), 0], ag_recv_u.at[g])
        for jump in (2, 1):
            for way in range(2):
                send_v(g, v, jump, way, jump)
        share(g, v)
    for g in range(len(groups)):
        for way in range(2):
            arrived(g, 2, way)
            row = at_v[-2 * signs[way]]
            if g in across[way]:
                send_v(g, row, 4, way, 2)
            send_v(g, row, 3, way, 1)
            share(g, row)
        for way in range(2):
            arrived(g, 1, way)
            share(g, at_v[-signs[way]])
    for g in range(len(groups)):
        for way in range(2):
            arrived(g, 3, way)
            share(g, wrap(v - 3 * signs[way]))
            if g in across[way]:
                arrived(g, 4, way)
                share(g, wrap(v - 4 * signs[way]))
    a_copy.wait()
    send_copy.wait()
    recv_copy.wait()
    shift_copy.wait()
    await_bytes(gathered.at[:, 0], ag_recv_s)

    tile = rows // 4
    depth = a_vmem.shape[1]

    def product(t, _):
        at = pl.ds(pl.multiple_of(t * tile, tile), tile)
        lhs = a_vmem[at, :]
        cols = gathered.shape[-1]
        one = jnp.dot(lhs, gathered[:, :, 0].reshape(depth, cols), preferred_element_type=F32)
        two = jnp.dot(lhs, gathered[:, :, 1].reshape(depth, cols), preferred_element_type=F32)
        schur = one * two
        sa[at, :] = schur[:, :LANES]
        sr[at, :] = pltpu.roll(schur[:, :LANES], PANEL, 1)
        sb[at, :] = schur[:, LANES:]
        return 0

    lax.fori_loop(0, 4, product, 0)

    low = lane_iota((1, LANES)) < PANEL

    def pack_lead(e, _):
        firsts, seconds = [], []
        for k in range(pair):
            firsts.append(sa[pl.ds(send_ref[0, e * per + k], 1), :])
            seconds.append(sr[pl.ds(send_ref[0, e * per + pair + k], 1), :])
        for k in range(pair):
            lead_out[e, pl.ds(k, 1), :] = jnp.where(low, firsts[k], seconds[k])
        return 0

    def send_to(e, source, target_ref, send, recv):
        @pl.when(e != me)
        def _():
            remote(source.at[e], target_ref.at[me], send, recv, e)

    def turn(start, i, span):
        e = start + i
        return jnp.where(e >= span, e - span, e)

    start_lead = lax.rem(me, n_lead)
    start_other = lax.rem(me, n - n_lead)

    def lead_first(i, _):
        send_to(turn(start_lead, i, n_lead), lead_out, lead_in, lead_send, lead_recv)
        return 0

    def lead_other(i, _):
        e = n_lead + turn(start_other, i, n - n_lead)
        send_to(e, lead_out, lead_in, lead_send, lead_recv)
        return 0

    ahead = min(2 * n_lead, n)
    lax.fori_loop(0, ahead, pack_lead, 0)
    lax.fori_loop(0, n_lead, lead_first, 0)
    lax.fori_loop(ahead, n, pack_lead, 0)
    lax.fori_loop(0, n - n_lead, lead_other, 0)
    lead_in[me] = lead_out[me]

    def pack_rest(e, _):
        parts = []
        for k in range(pair):
            one = send_ref[0, e * per + k]
            two = send_ref[0, e * per + pair + k]
            parts.append((
                sb[pl.ds(one, 1), :], sb[pl.ds(two, 1), :],
                sr[pl.ds(one, 1), :], sa[pl.ds(two, 1), :],
            ))
        for k in range(pair):
            one, two, left, right = parts[k]
            rest_f[e, pl.ds(k, 1), :] = one
            rest_f[e, pl.ds(pair + k, 1), :] = two
            rest_f[e, pl.ds(2 * pair + k, 1), :] = jnp.where(low, left, right)
        return 0

    rest_f[:, 3 * pair :, :] = jnp.zeros((n, 16 - 3 * pair, LANES), F32)
    lax.fori_loop(0, n, pack_rest, 0)

    def quantize(i, _):
        at = pl.ds(i * 8, 8)
        values = rest_f[at]
        largest = jnp.max(jnp.abs(values), axis=1, keepdims=True)
        power = jnp.floor(jnp.log2(jnp.maximum(largest, 1e-30))) + 1.0
        scale = Q_MAX / jnp.exp2(power)
        coded = jnp.clip(jnp.round(values * scale), -Q_MAX, Q_MAX)
        spot = lax.broadcasted_iota(jnp.int32, values.shape, 1)
        coded = jnp.where(spot == 3 * pair, power, coded)
        rest_out[at] = coded.astype(jnp.int32).astype(jnp.int16)
        return 0

    lax.fori_loop(0, n // 8, quantize, 0)

    chunks = 8
    span = n // chunks
    my_chunk = lax.div(me, span)

    def send_rest(i, _):
        send_to(turn(me, i, n), rest_out, rest_in, rest_send, rest_recv.at[my_chunk])
        return 0

    relays_first = (me < n_lead) | ((x == 0) & (core == 0))

    @pl.when(jnp.logical_not(relays_first))
    def _():
        lax.fori_loop(1, n, send_rest, 0)

    magic = -(-65536 // per)
    assert all((j * magic) >> 16 == j // per for j in range(rows))

    def find_slots(i, _):
        for k in range(8):
            slot = recv_ref[0, i * 8 + k]
            source = lax.shift_right_logical(slot * magic, 16)
            slots[0, i * 8 + k] = slot + (16 - per) * source
        return 0


    flat_a = both_a.reshape(n * 16, LANES)
    flat_b = rest_g.reshape(n * 16, LANES)

    def take(source, start):
        return jnp.concatenate(
            [source[pl.ds(slots[0, start + k], 1), :] for k in range(8)], axis=0
        )

    def take_leads():
        await_bytes(lead_in.at[0 : n - 1], lead_recv)

        def spread_lead(i, _):
            at = pl.ds(i * 8, 8)
            values = lead_in[at]
            both_a[at, 0:pair] = values
            both_a[at, pair : 2 * pair] = pltpu.roll(values, PANEL, 2)
            return 0

        lax.fori_loop(0, n // 8, spread_lead, 0)

    hp = PANEL // 2
    group = 2 * side
    levels = -(-n_lead // group)

    @pl.when(me < n_lead)
    def _():
        lax.fori_loop(0, PANEL // 8, find_slots, 0)
        take_leads()

        def first(i, _):
            first_rows[pl.ds(pl.multiple_of(i * 8, 8), 8), :] = take(flat_a, i * 8)
            return 0

        lax.fori_loop(0, PANEL // 8, first, 0)
        packed = jnp.where(
            low, first_rows[0:hp, :], pltpu.roll(first_rows[hp:PANEL, :], PANEL, 1)
        )
        leading_src[...] = packed
        leading[me] = packed
        for i in sorted(range(1, side), key=lambda i: -min(i, side - i)):
            target = (wrap(y + i) * side + x) * 2 + core
            remote(leading_src, leading.at[me], tree_send1, tree_recv1.at[y], target)

    def relay(m, e):
        @pl.when(y != m)
        def _():
            await_bytes(leading.at[0], tree_recv1.at[m])

        for i in sorted(range(1, side), key=lambda i: -min(i, side - i)):
            target = (y * side + wrap(x + i)) * 2 + core
            remote(leading.at[e], leading.at[e], tree_send2.at[m], tree_recv2.at[e], target)
        remote(leading.at[e], leading.at[e], tree_send3.at[e], tree_recv3.at[e], sibling)

    @pl.when((x == 0) & (core == 0))
    def _():
        relay(0, 0)

    @pl.when(relays_first)
    def _():
        lax.fori_loop(1, n, send_rest, 0)

    rest_in[me] = rest_out[me]

    for m in range(levels):
        e = m * group + 2 * x + core

        @pl.when((e < n_lead) & (e > 0))
        def _(m=m, e=e):
            relay(m, e)

    lax.fori_loop(0, rows // 8, find_slots, 0)

    @pl.when(me >= n_lead)
    def _():
        take_leads()

    def pass_on(e):
        await_bytes(leading.at[0], tree_recv2.at[e])
        remote(leading.at[e], leading.at[e], tree_send3.at[e], tree_recv3.at[e], sibling)

    @pl.when((x != 0) & (core == 0))
    def _():
        pass_on(0)

    @pl.when(core == 1)
    def _():
        await_bytes(leading.at[0], tree_recv3.at[0])

    eliminate_block(leading[0], shift_ref, work, lower_ref, pivots_ref)

    for m in range(levels):
        for i in range(1, side):
            e = m * group + 2 * wrap(x + i) + core

            @pl.when((e < n_lead) & (e > 0))
            def _(e=e):
                pass_on(e)

    def from_sibling(e, _):
        @pl.when(lax.rem(e, 2) != core)
        def _():
            await_bytes(leading.at[0], tree_recv3.at[e])

        return 0

    lax.fori_loop(1, n_lead, from_sibling, 0)

    def spread_rest(i, _):
        at = pl.ds(i * 8, 8)
        coded = rest_in[at].astype(jnp.int32).astype(F32)
        power = coded[:, 3 * pair : 3 * pair + 1]
        values = coded * (jnp.exp2(power) / Q_MAX)
        rest_g[at] = values
        mid = values[:, 2 * pair : 3 * pair]
        kept = lane_iota(mid.shape) < PANEL
        both_a[at, 0:pair] = jnp.where(kept, both_a[at, 0:pair], pltpu.roll(mid, PANEL, 2))
        both_a[at, pair : 2 * pair] = jnp.where(kept, both_a[at, pair : 2 * pair], mid)
        return 0

    for chunk in range(chunks):
        at = chunk * span

        @pl.when(my_chunk == chunk)
        def _(chunk=chunk, at=at):
            await_bytes(rest_in.at[at : at + span - 1], rest_recv.at[chunk])

        @pl.when(my_chunk != chunk)
        def _(chunk=chunk, at=at):
            await_bytes(rest_in.at[at : at + span], rest_recv.at[chunk])

        lax.fori_loop(at // 8, (at + span) // 8, spread_rest, 0)

    def place(i, _):
        at = pl.ds(pl.multiple_of(i * 8, 8), 8)
        stored_a[at, :] = take(flat_a, i * 8)
        stored_b[at, :] = take(flat_b, i * 8)
        return 0

    lax.fori_loop(0, rows // 8, place, 0)

    await_bytes(gathered.at[0 : side - 1, 0], ag_send.at[0])
    await_bytes(gathered.at[0 : side * (side - 1), 0], ag_send.at[1])
    await_bytes(gathered.at[:, 0], ag_send.at[2])
    await_bytes(lead_out.at[0 : n - 1], lead_send)
    await_bytes(rest_out.at[0 : n - 1], rest_send)

    @pl.when(me < n_lead)
    def _():
        await_bytes(leading.at[0 : side - 1], tree_send1)

    for m in range(levels):
        e = m * group + 2 * x + core

        @pl.when(e < n_lead)
        def _(m=m):
            await_bytes(leading.at[0 : side - 1], tree_send2.at[m])

    def to_sibling(e, _):
        @pl.when(lax.rem(e, 2) == core)
        def _():
            await_bytes(leading.at[0], tree_send3.at[e])

        return 0

    lax.fori_loop(0, n_lead, to_sibling, 0)


def eliminate_block(head, shift_ref, work, lower_ref, pivots_ref):
    turned = pltpu.roll(head, PANEL, 1)
    block = jnp.concatenate([head, turned], axis=0)
    r = lax.broadcasted_iota(jnp.int32, block.shape, 0)
    c = lane_iota(block.shape)
    inside = c < PANEL
    strict = jnp.where((r > c) & inside, block, 0.0)
    pad = jnp.concatenate([strict, jnp.zeros_like(strict)], axis=0)
    mirrored = jnp.where((r >= c) & inside, block, 0.0) + pad.T[:PANEL, :]
    magnitude = jnp.sum(jnp.abs(mirrored), axis=0, keepdims=True)
    shift = shift_ref[...].reshape(1, PANEL)
    diagonal = magnitude + jnp.concatenate([shift, shift], axis=1)
    start = jnp.where(r == c, diagonal, mirrored)
    work[...] = jnp.where(inside, start, jnp.where(r == c - PANEL, 1.0, 0.0))
    lower_ref[...] = jnp.zeros_like(block)

    lane = lane_iota((1, LANES))

    def pick(values, mask):
        return jnp.sum(jnp.where(mask, values, 0.0), axis=1, keepdims=True)

    def eliminate(i, pivots):
        j = 2 * i
        matrix = work[...]
        row0 = work[pl.ds(j, 1), :]
        row1 = work[pl.ds(j + 1, 1), :]
        column0 = pick(matrix, c == j)
        column1 = pick(matrix, c == j + 1)
        pivot0 = pick(row0, lane == j)
        beside = pick(row0, lane == j + 1)
        under = pick(row1, lane == j)
        corner = pick(row1, lane == j + 1)
        inverse0 = 1.0 / pivot0
        ratio = under * inverse0
        below0 = jnp.where(r > j, column0 * inverse0, 0.0)
        row1 = row1 - ratio * row0
        pivot1 = corner - ratio * beside
        below1 = jnp.where(r > j + 1, (column1 - below0 * beside) * (1.0 / pivot1), 0.0)
        work[...] = matrix - below0 * row0 - below1 * row1
        new0 = below0 + jnp.where(r == j, 1.0, 0.0)
        new1 = below1 + jnp.where(r == j + 1, 1.0, 0.0)
        lower_ref[...] += jnp.where(c == j, new0, jnp.where(c == j + 1, new1, 0.0))
        return jnp.where(lane == j, pivot0, jnp.where(lane == j + 1, pivot1, pivots))

    pivots_ref[...] = lax.fori_loop(0, PANEL // 2, eliminate, jnp.ones((1, LANES), F32))


def exchange(n, n_lead, a_rows, xa, za, send_order, recv_order, shift):
    rows, depth = a_rows.shape
    cols = xa.shape[1]
    share = xa.shape[0]
    per = rows // n
    pair = per // 2
    side = math.isqrt(n // 2)
    hp = PANEL // 2
    dma = pltpu.SemaphoreType.DMA
    hbm = pl.BlockSpec(memory_space=pltpu.HBM)
    vmem = pl.BlockSpec(memory_space=pltpu.VMEM)
    levels = -(-n_lead // (2 * side))
    n_groups = len(u_groups(side))
    return pl.pallas_call(
        functools.partial(exchange_kernel, n, n_lead),
        out_shape=(
            jax.ShapeDtypeStruct((rows, LANES), F32),
            jax.ShapeDtypeStruct((rows, LANES), F32),
            jax.ShapeDtypeStruct((n_lead, hp, LANES), F32),
            jax.ShapeDtypeStruct((PANEL, LANES), F32),
            jax.ShapeDtypeStruct((PANEL, LANES), F32),
            jax.ShapeDtypeStruct((1, LANES), F32),
        ),
        in_specs=[hbm] * 6,
        out_specs=(vmem,) * 6,
        scratch_shapes=[
            pltpu.VMEM((rows, depth), BF16),
            pltpu.VMEM((n // 2, 2, 2, share, cols), BF16),
            pltpu.VMEM((rows, LANES), F32),
            pltpu.VMEM((rows, LANES), F32),
            pltpu.VMEM((rows, LANES), F32),
            pltpu.VMEM((n, pair, LANES), F32),
            pltpu.VMEM((n, 16, LANES), F32),
            pltpu.VMEM((n, 16, LANES), jnp.int16),
            pltpu.VMEM((n, pair, LANES), F32),
            pltpu.VMEM((n, 16, LANES), jnp.int16),
            pltpu.VMEM((n, 16, LANES), F32),
            pltpu.VMEM((n, 16, LANES), F32),
            pltpu.VMEM((PANEL, LANES), F32),
            pltpu.VMEM((hp, LANES), F32),
            pltpu.VMEM((PANEL,), F32),
            pltpu.SMEM((1, rows), jnp.int32),
            pltpu.SMEM((1, rows), jnp.int32),
            pltpu.SMEM((1, rows), jnp.int32),
            dma, dma((2,)), dma((3,)), dma((3,)), dma((n_groups,)), dma((2, 4, n_groups)), dma,
            dma, dma, dma, dma((8,)),
            dma, dma((levels,)), dma((n_lead,)), dma((side,)), dma((n_lead,)), dma((n_lead,)),
        ],
        compiler_params=pltpu.CompilerParams(
            collective_id=0, has_side_effects=True, vmem_limit_bytes=48 * 1024 * 1024
        ),
    )(*(pltpu.with_memory_space_constraint(o, pltpu.HBM) for o in (
        a_rows, xa, za, send_order, recv_order, shift
    )))


def two_parts(values):
    high = values.astype(BF16)
    return high, (values - high.astype(F32)).astype(BF16)


def left_stack(twice):
    high, mid = two_parts(twice)
    return jnp.concatenate([high, mid], axis=1)


def right_stack(twice):
    high, mid = two_parts(twice)
    once = jnp.where(lane_iota(twice.shape) < PANEL, high.astype(F32), mid.astype(F32))
    once = once.astype(BF16)
    return jnp.concatenate([once, once], axis=1)


def dot_nt(a, b):
    return lax.dot_general(a, b, (((1,), (1,)), ((), ())), preferred_element_type=F32)


def finish_kernel(
    a_ref, b_ref, leading, work, lower_ref, pivot_ref, resident_ref,
    factored_ref, updated_ref, pivots_ref,
    inverse_ref, tail_ref,
):
    step = pl.program_id(0)
    me = lax.axis_index("wide")
    tile = a_ref.shape[0]

    @pl.when(step == 0)
    def _():
        final = work[...]
        inside = lane_iota(final.shape) < PANEL
        pivots_ref[...] = pivot_ref[...][0, :PANEL]
        inverse = jnp.where(inside, pltpu.roll(final, PANEL, 1), final)
        inverse_ref[0:PANEL, :] = right_stack(inverse)
        inverse_ref[PANEL:, :] = jnp.zeros_like(inverse_ref[PANEL:, :])
        blocks = leading[...]
        keep = lane_iota(blocks.shape) < PANEL
        other = pltpu.roll(blocks, PANEL, 2)
        top = jnp.where(keep, blocks, other)
        bottom = jnp.where(keep, other, blocks)
        full = jnp.concatenate([top, bottom], axis=1)
        full = full.reshape(full.shape[0] * PANEL, LANES)
        tail = dot_nt(left_stack(full), inverse_ref[...])
        tail = tail + pltpu.roll(tail, PANEL, 1)
        place = lax.broadcasted_iota(jnp.int32, tail.shape, 0)
        tail_ref[...] = right_stack(jnp.where(place < PANEL, 0.0, tail))

    a = a_ref[...]
    lanes = lane_iota(a.shape)
    local = lax.broadcasted_iota(jnp.int32, a.shape, 0) + step * tile
    low = lanes < PANEL
    lead = jnp.where(low, a, pltpu.roll(a, PANEL, 1))
    scaled = dot_nt(left_stack(lead), inverse_ref[...])
    panel = scaled / pivot_ref[...]
    is_top = (local < PANEL) & (me == 0)
    fill = tile // PANEL
    lower = jnp.concatenate([lower_ref[...]] * fill, axis=0)
    panel = jnp.where(is_top, lower, panel)
    update = dot_nt(left_stack(panel + pltpu.roll(panel, PANEL, 1)), tail_ref[...])
    cols = b_ref.shape[1] + a.shape[1]

    def kept(values):
        rows_at = lax.broadcasted_iota(jnp.int32, values.shape, 0) + step * tile
        return jnp.where((rows_at < PANEL) & (me == 0), 0.0, values)

    factored_ref[:, :LANES] = jnp.where(low, panel, a - kept(update[:, :LANES]))
    factored_ref[:, LANES:] = b_ref[...] - kept(update[:, LANES:cols])
    updated_ref[...] = (resident_ref[...].astype(F32) - kept(update[:, cols:])).astype(BF16)


def finish(stored_a, stored_b, leading, work, lower, pivots, resident):
    rows = stored_a.shape[0]
    tile = 256
    width = resident.shape[1]
    cols = stored_a.shape[1] + stored_b.shape[1]
    n_lead = leading.shape[0]
    row_spec = lambda w: pl.BlockSpec((tile, w), lambda i: (i, 0))
    whole = lambda shape: pl.BlockSpec(shape, lambda i: (0,) * len(shape))
    return pl.pallas_call(
        finish_kernel,
        grid=(rows // tile,),
        out_shape=(
            jax.ShapeDtypeStruct((rows, cols), F32),
            jax.ShapeDtypeStruct((rows, width), BF16),
            jax.ShapeDtypeStruct((PANEL,), F32),
        ),
        in_specs=[
            row_spec(LANES), row_spec(LANES), whole(leading.shape), whole(work.shape),
            whole(lower.shape), whole(pivots.shape), row_spec(width),
        ],
        out_specs=(row_spec(cols), row_spec(width), whole((PANEL,))),
        scratch_shapes=[
            pltpu.VMEM((LANES, 2 * LANES), BF16),
            pltpu.VMEM((n_lead * PANEL, 2 * LANES), BF16),
        ],
        compiler_params=pltpu.CompilerParams(vmem_limit_bytes=32 * 1024 * 1024),
    )(stored_a, stored_b, leading, work, lower, pivots, resident)


def on_device(n, a_rows, xa_panel, za_panel, send_order, recv_order, shift, resident):
    needed = xa_panel.shape[1] + resident.shape[1]
    n_lead = -(-needed // PANEL)
    stored_a, stored_b, leading, work, lower, pivots = exchange(
        n, n_lead, a_rows, xa_panel, za_panel, send_order, recv_order, shift
    )
    return finish(stored_a, stored_b, leading, work, lower, pivots, resident)


def solution(mesh):
    spread = P(("parts", "wide"), None)
    return jax.shard_map(
        functools.partial(on_device, mesh.shape["wide"]),
        mesh=mesh,
        in_specs=(spread, spread, spread, spread, spread, P("parts"), spread),
        out_specs=(spread, spread, P("parts")),
        check_vma=False,
    )
```

time: 103 us -> 86.8 us (0.84)
  the two profiles are of different devices: /device:TPU:513 before, /device:TPU:529 now
where the time goes in v2:
time: 86.8 us; the launch traced here: 86.7 us
  Pallas kernels  86.1 us (99%)
    pallas_call x1, Pallas kernels, exchange(): pl.pallas_call(functools.partial(exchange_kernel, n, n_lead), out_shape=(...  81.3 us
    pallas_call x1, Pallas kernels, finish(): pl.pallas_call(finish_kernel, grid=(rows // tile,), out_shape=(jax.ShapeD...  4.74 us

profile of v2, /device:TPU:529, one launch (start us, length us, event | category | flops | bytes accessed | tf_op | source)
XLA Modules:
  0.0 86.7 jit_solution(1553037819442645375)
XLA Ops:
  0.6 0.0 copy-start
  0.6 81.3 %shard_map.94 = (f32[1280,128]{1,0:T(8,128)S(1)}, f32[1280,128]{1,0:T(8,128)S(1)}, f32[20,32,128]{2,1,0:T(8,128)S(1)}, f32[64,128]{1,0:T(8,128)S(1)}, f32[64,128]{1,0:T(8,128)S(1)}, /*index=5*/f32[1,128]{1,0:T(1,128)S(1)}) custom-call(bf16[1280,2048]{1,0:T(8,128)(2,1)} %a_hbm.1, bf16[16,256]{1,0:T(8,128)(2,1)} %xa_hbm.1, bf16[16,256]{1,0:T(8,128)(2,1)} %za_hbm.1, ...), custom_call_target="tpu_custom_call" | custom-call | tf_op jit(solution)/shard_map/pallas_call | solution.py:496
  82.0 0.0 copy-done
  82.0 4.7 %shard_map.95 = (f32[1280,256]{1,0:T(8,128)}, bf16[1280,1024]{1,0:T(8,128)(2,1)}, f32[64]{0:T(128)}) custom-call(f32[1280,128]{1,0:T(8,128)S(1)} %get-tuple-element.9.a_ref, f32[1280,128]{1,0:T(8,128)S(1)} %get-tuple-element.10.b_ref, f32[20,32,128]{2,1,0:T(8,128)S(1)} %get-tuple-element.11.leading, f32[64,128]{1,0:T(8,128)S(1)} %get-tuple-element.12.work, ...), custom_call_target="tpu_custom_call" | custom-call | tf_op jit(solution)/shard_map/pallas_call | solution.py:620
Async XLA Ops:
  0.6 81.4 %copy-start = (bf16[1280,1024]{1,0:T(8,128)(2,1)S(1)}, bf16[1280,1024]{1,0:T(8,128)(2,1)}, u32[]{:S(2)}) copy-start(bf16[1280,1024]{1,0:T(8,128)(2,1)} %resident_ref.1) | copy-start | bytes 7864324

commit v3 on v2

--- a/solution.py
+++ b/solution.py
@@ -9,6 +9,7 @@
 from jax.sharding import PartitionSpec as P
 
 PANEL = 64
+SPREAD = 45
 LANES = 128
 Q_MAX = 32767.0
 F32 = jnp.float32
@@ -185,28 +186,104 @@
         def _():
             remote(source.at[e], target_ref.at[me], send, recv, e)
 
-    def turn(start, i, span):
-        e = start + i
-        return jnp.where(e >= span, e - span, e)
+    def mixed(i):
+        return lax.rem(me + i * SPREAD, n)
+
+    def lead_first(i, _):
+        e = start_lead + i
+        e = jnp.where(e >= n_lead, e - n_lead, e)
+
+        @pl.when(e != 0)
+        def _():
+            send_to(e, lead_out, lead_in, lead_send, lead_recv)
+
+        return 0
+
+    def lead_other(i, _):
+        e = mixed(i)
+
+        @pl.when(e >= n_lead)
+        def _():
+            send_to(e, lead_out, lead_in, lead_send, lead_recv)
+
+        return 0
 
     start_lead = lax.rem(me, n_lead)
-    start_other = lax.rem(me, n - n_lead)
-
-    def lead_first(i, _):
-        send_to(turn(start_lead, i, n_lead), lead_out, lead_in, lead_send, lead_recv)
-        return 0
-
-    def lead_other(i, _):
-        e = n_lead + turn(start_other, i, n - n_lead)
-        send_to(e, lead_out, lead_in, lead_send, lead_recv)
-        return 0
-
-    ahead = min(2 * n_lead, n)
-    lax.fori_loop(0, ahead, pack_lead, 0)
+    assert math.gcd(SPREAD, n) == 1
+    lax.fori_loop(0, n_lead, pack_lead, 0)
+    send_to(0, lead_out, lead_in, lead_send, lead_recv)
+    lax.fori_loop(n_lead, n, pack_lead, 0)
     lax.fori_loop(0, n_lead, lead_first, 0)
-    lax.fori_loop(ahead, n, pack_lead, 0)
-    lax.fori_loop(0, n - n_lead, lead_other, 0)
+    lax.fori_loop(1, n, lead_other, 0)
     lead_in[me] = lead_out[me]
+
+    magic = -(-65536 // per)
+    assert all((j * magic) >> 16 == j // per for j in range(rows))
+
+    def find_slots(i, _):
+        for k in range(8):
+            slot = recv_ref[0, i * 8 + k]
+            source = lax.shift_right_logical(slot * magic, 16)
+            slots[0, i * 8 + k] = slot + (16 - per) * source
+        return 0
+
+
+    flat_a = both_a.reshape(n * 16, LANES)
+    flat_b = rest_g.reshape(n * 16, LANES)
+
+    def take(source, start):
+        return jnp.concatenate(
+            [source[pl.ds(slots[0, start + k], 1), :] for k in range(8)], axis=0
+        )
+
+    def take_leads():
+        await_bytes(lead_in.at[0 : n - 1], lead_recv)
+
+        def spread_lead(i, _):
+            at = pl.ds(i * 8, 8)
+            values = lead_in[at]
+            both_a[at, 0:pair] = values
+            both_a[at, pair : 2 * pair] = pltpu.roll(values, PANEL, 2)
+            return 0
+
+        lax.fori_loop(0, n // 8, spread_lead, 0)
+
+    hp = PANEL // 2
+    group = 2 * side
+    levels = -(-n_lead // group)
+
+    def publish():
+        lax.fori_loop(0, PANEL // 8, find_slots, 0)
+        take_leads()
+
+        def first(i, _):
+            first_rows[pl.ds(pl.multiple_of(i * 8, 8), 8), :] = take(flat_a, i * 8)
+            return 0
+
+        lax.fori_loop(0, PANEL // 8, first, 0)
+        packed = jnp.where(
+            low, first_rows[0:hp, :], pltpu.roll(first_rows[hp:PANEL, :], PANEL, 1)
+        )
+        leading_src[...] = packed
+        leading[me] = packed
+        for i in sorted(range(1, side), key=lambda i: -min(i, side - i)):
+            target = (wrap(y + i) * side + x) * 2 + core
+            remote(leading_src, leading.at[me], tree_send1, tree_recv1.at[y], target)
+
+    def relay(m, e):
+        @pl.when(y != m)
+        def _():
+            await_bytes(leading.at[0], tree_recv1.at[m])
+
+        for i in sorted(range(1, side), key=lambda i: -min(i, side - i)):
+            target = (y * side + wrap(x + i)) * 2 + core
+            remote(leading.at[e], leading.at[e], tree_send2.at[m], tree_recv2.at[e], target)
+        remote(leading.at[e], leading.at[e], tree_send3.at[e], tree_recv3.at[e], sibling)
+
+    @pl.when(me == 0)
+    def _():
+        publish()
+        relay(0, 0)
 
     def pack_rest(e, _):
         parts = []
@@ -246,88 +323,48 @@
     my_chunk = lax.div(me, span)
 
     def send_rest(i, _):
-        send_to(turn(me, i, n), rest_out, rest_in, rest_send, rest_recv.at[my_chunk])
-        return 0
-
-    relays_first = (me < n_lead) | ((x == 0) & (core == 0))
+        send_to(mixed(i), rest_out, rest_in, rest_send, rest_recv.at[my_chunk])
+        return 0
+
+    on_path = (x == 0) & (core == 0)
+    relays_first = (me < n_lead) | on_path
 
     @pl.when(jnp.logical_not(relays_first))
     def _():
         lax.fori_loop(1, n, send_rest, 0)
 
-    magic = -(-65536 // per)
-    assert all((j * magic) >> 16 == j // per for j in range(rows))
-
-    def find_slots(i, _):
-        for k in range(8):
-            slot = recv_ref[0, i * 8 + k]
-            source = lax.shift_right_logical(slot * magic, 16)
-            slots[0, i * 8 + k] = slot + (16 - per) * source
-        return 0
-
-
-    flat_a = both_a.reshape(n * 16, LANES)
-    flat_b = rest_g.reshape(n * 16, LANES)
-
-    def take(source, start):
-        return jnp.concatenate(
-            [source[pl.ds(slots[0, start + k], 1), :] for k in range(8)], axis=0
-        )
-
-    def take_leads():
-        await_bytes(lead_in.at[0 : n - 1], lead_recv)
-
-        def spread_lead(i, _):
-            at = pl.ds(i * 8, 8)
-            values = lead_in[at]
-            both_a[at, 0:pair] = values
-            both_a[at, pair : 2 * pair] = pltpu.roll(values, PANEL, 2)
-            return 0
-
-        lax.fori_loop(0, n // 8, spread_lead, 0)
-
-    hp = PANEL // 2
-    group = 2 * side
-    levels = -(-n_lead // group)
-
-    @pl.when(me < n_lead)
-    def _():
-        lax.fori_loop(0, PANEL // 8, find_slots, 0)
+    @pl.when(on_path & (me > 0))
+    def _():
+        relay(0, 0)
+
+    @pl.when((me < n_lead) & (me > 0))
+    def _():
+        publish()
+
+    @pl.when(relays_first)
+    def _():
+        lax.fori_loop(1, n, send_rest, 0)
+
+    rest_in[me] = rest_out[me]
+    lax.fori_loop(0, rows // 8, find_slots, 0)
+
+    @pl.when(me >= n_lead)
+    def _():
         take_leads()
 
-        def first(i, _):
-            first_rows[pl.ds(pl.multiple_of(i * 8, 8), 8), :] = take(flat_a, i * 8)
-            return 0
-
-        lax.fori_loop(0, PANEL // 8, first, 0)
-        packed = jnp.where(
-            low, first_rows[0:hp, :], pltpu.roll(first_rows[hp:PANEL, :], PANEL, 1)
-        )
-        leading_src[...] = packed
-        leading[me] = packed
-        for i in sorted(range(1, side), key=lambda i: -min(i, side - i)):
-            target = (wrap(y + i) * side + x) * 2 + core
-            remote(leading_src, leading.at[me], tree_send1, tree_recv1.at[y], target)
-
-    def relay(m, e):
-        @pl.when(y != m)
-        def _():
-            await_bytes(leading.at[0], tree_recv1.at[m])
-
-        for i in sorted(range(1, side), key=lambda i: -min(i, side - i)):
-            target = (y * side + wrap(x + i)) * 2 + core
-            remote(leading.at[e], leading.at[e], tree_send2.at[m], tree_recv2.at[e], target)
+    def pass_on(e):
+        await_bytes(leading.at[0], tree_recv2.at[e])
         remote(leading.at[e], leading.at[e], tree_send3.at[e], tree_recv3.at[e], sibling)
 
-    @pl.when((x == 0) & (core == 0))
-    def _():
-        relay(0, 0)
-
-    @pl.when(relays_first)
-    def _():
-        lax.fori_loop(1, n, send_rest, 0)
-
-    rest_in[me] = rest_out[me]
+    @pl.when((x != 0) & (core == 0))
+    def _():
+        pass_on(0)
+
+    @pl.when(core == 1)
+    def _():
+        await_bytes(leading.at[0], tree_recv3.at[0])
+
+    eliminate_block(leading[0], shift_ref, work, lower_ref, pivots_ref)
 
     for m in range(levels):
         e = m * group + 2 * x + core
@@ -335,43 +372,6 @@
         @pl.when((e < n_lead) & (e > 0))
         def _(m=m, e=e):
             relay(m, e)
-
-    lax.fori_loop(0, rows // 8, find_slots, 0)
-
-    @pl.when(me >= n_lead)
-    def _():
-        take_leads()
-
-    def pass_on(e):
-        await_bytes(leading.at[0], tree_recv2.at[e])
-        remote(leading.at[e], leading.at[e], tree_send3.at[e], tree_recv3.at[e], sibling)
-
-    @pl.when((x != 0) & (core == 0))
-    def _():
-        pass_on(0)
-
-    @pl.when(core == 1)
-    def _():
-        await_bytes(leading.at[0], tree_recv3.at[0])
-
-    eliminate_block(leading[0], shift_ref, work, lower_ref, pivots_ref)
-
-    for m in range(levels):
-        for i in range(1, side):
-            e = m * group + 2 * wrap(x + i) + core
-
-            @pl.when((e < n_lead) & (e > 0))
-            def _(e=e):
-                pass_on(e)
-
-    def from_sibling(e, _):
-        @pl.when(lax.rem(e, 2) != core)
-        def _():
-            await_bytes(leading.at[0], tree_recv3.at[e])
-
-        return 0
-
-    lax.fori_loop(1, n_lead, from_sibling, 0)
 
     def spread_rest(i, _):
         at = pl.ds(i * 8, 8)
@@ -398,6 +398,14 @@
 
         lax.fori_loop(at // 8, (at + span) // 8, spread_rest, 0)
 
+    for m in range(levels):
+        for i in range(1, side):
+            e = m * group + 2 * wrap(x + i) + core
+
+            @pl.when((e < n_lead) & (e > 0))
+            def _(e=e):
+                pass_on(e)
+
     def place(i, _):
         at = pl.ds(pl.multiple_of(i * 8, 8), 8)
         stored_a[at, :] = take(flat_a, i * 8)
@@ -405,6 +413,15 @@
         return 0
 
     lax.fori_loop(0, rows // 8, place, 0)
+
+    def from_sibling(e, _):
+        @pl.when(lax.rem(e, 2) != core)
+        def _():
+            await_bytes(leading.at[0], tree_recv3.at[e])
+
+        return 0
+
+    lax.fori_loop(1, n_lead, from_sibling, 0)
 
     await_bytes(gathered.at[0 : side - 1, 0], ag_send.at[0])
     await_bytes(gathered.at[0 : side * (side - 1), 0], ag_send.at[1])

time: 86.8 us -> 80 us (0.922)
  the two profiles are of different devices: /device:TPU:529 before, /device:TPU:513 now
where the time goes in v3:
time: 80 us; the launch traced here: 79.9 us
  Pallas kernels  79.2 us (99%)
    pallas_call x1, Pallas kernels, exchange(): pl.pallas_call(functools.partial(exchange_kernel, n, n_lead), out_shape=(...  74.5 us
    pallas_call x1, Pallas kernels, finish(): pl.pallas_call(finish_kernel, grid=(rows // tile,), out_shape=(jax.ShapeD...  4.73 us

profile of v3, /device:TPU:513, one launch (start us, length us, event | category | flops | bytes accessed | tf_op | source)
XLA Modules:
  0.0 79.9 jit_solution(8403049411185248844)
XLA Ops:
  0.6 0.0 copy-start
  0.6 74.5 %shard_map.94 = (f32[1280,128]{1,0:T(8,128)S(1)}, f32[1280,128]{1,0:T(8,128)S(1)}, f32[20,32,128]{2,1,0:T(8,128)S(1)}, f32[64,128]{1,0:T(8,128)S(1)}, f32[64,128]{1,0:T(8,128)S(1)}, /*index=5*/f32[1,128]{1,0:T(1,128)S(1)}) custom-call(bf16[1280,2048]{1,0:T(8,128)(2,1)} %a_hbm.1, bf16[16,256]{1,0:T(8,128)(2,1)} %xa_hbm.1, bf16[16,256]{1,0:T(8,128)(2,1)} %za_hbm.1, ...), custom_call_target="tpu_custom_call" | custom-call | tf_op jit(solution)/shard_map/pallas_call | solution.py:513
  75.1 0.0 copy-done
  75.1 4.7 %shard_map.95 = (f32[1280,256]{1,0:T(8,128)}, bf16[1280,1024]{1,0:T(8,128)(2,1)}, f32[64]{0:T(128)}) custom-call(f32[1280,128]{1,0:T(8,128)S(1)} %get-tuple-element.9.a_ref, f32[1280,128]{1,0:T(8,128)S(1)} %get-tuple-element.10.b_ref, f32[20,32,128]{2,1,0:T(8,128)S(1)} %get-tuple-element.11.leading, f32[64,128]{1,0:T(8,128)S(1)} %get-tuple-element.12.work, ...), custom_call_target="tpu_custom_call" | custom-call | tf_op jit(solution)/shard_map/pallas_call | solution.py:637
Async XLA Ops:
  0.6 74.5 %copy-start = (bf16[1280,1024]{1,0:T(8,128)(2,1)S(1)}, bf16[1280,1024]{1,0:T(8,128)(2,1)}, u32[]{:S(2)}) copy-start(bf16[1280,1024]{1,0:T(8,128)(2,1)} %resident_ref.1) | copy-start | bytes 7864324
